TPU v7x, 32 devices: a whole 2x2x4 slice. The times are simulated.
32 devices in a mesh: dp: 4 (over y, core), expert: 4 (over z), tensor: 2 (over x).
Axes of the slice: x: 2, y: 2, z: 4, core: 2. Of those that a mesh axis runs over, the one named last changes fastest.
Arguments:
- router_input: bfloat16 [1024, 2048], P(('dp', 'expert'), 'tensor'), may hold values from -6 to 6
- router_weight: bfloat16 [2048, 8], replicated, may hold values from -0.125 to 0.125
- expert_ids: int32 [1024, 2], P(('dp', 'expert', 'tensor')), may hold values from 0 to 7, all different within a row; in each aligned block of 32 rows (0 to 31, 32 to 63, ...) at most 9 rows name the same one
- down_weight: bfloat16 [61440, 2048], P(('expert', 'tensor')), may hold values from -0.0625 to 0.0625
- hidden: bfloat16 [4, 72, 61440], P('dp', None, ('expert', 'tensor')), may hold values from -6 to 6
- grad_output: bfloat16 [1024, 2048], P(('dp', 'expert', 'tensor')), may hold values from -4 to 4
Outputs:
- weight_grad: bfloat16 [61440, 2048], P(('expert', 'tensor', 'dp'))
- hidden_grad: bfloat16 [4, 72, 61440], P('dp', None, ('expert', 'tensor'))
- router_grad: float32 [2048, 8], replicated
- input_grad: bfloat16 [1024, 2048], P(('dp', 'expert', 'tensor'))
Inputs may be any that keep to these rules, and one draw needn't show every extreme that they name: `expert_ids`: each row names 2 different experts. Within the 32 rows of one device no expert is named more than 9 times, and some device's rows name some expert exactly 9 times.
All inputs are finite; a program needn't handle non-finite values.
Results may differ from a plain program's by a relative error of at most 0.018.
Values may be sent and summed in bfloat16 or wider, within the bound.
A program may use at most 192 MiB of HBM per device.

v0:
```python
import jax
import jax.numpy as jnp
from jax import lax
from jax.sharding import PartitionSpec as P


def per_device(router_input, router_weight, expert_ids, down_weight, hidden, grad_output):
    token_rows = grad_output.shape[0]
    model_width = grad_output.shape[1]
    expert_count = router_weight.shape[1]
    choose_count = expert_ids.shape[1]
    expert_ranks = lax.axis_size("expert")
    tensor_ranks = lax.axis_size("tensor")
    sources = expert_ranks * tensor_ranks
    spread = sources // expert_count
    capacity = hidden.shape[1] // sources
    full_input = lax.all_to_all(router_input, "tensor", split_axis=0, concat_axis=1, tiled=True)
    logits = jnp.dot(full_input, router_weight, preferred_element_type=jnp.float32)
    labels = jnp.arange(expert_count, dtype=jnp.int32)
    onehot_int = (expert_ids[:, :, None] == labels).astype(jnp.int32)
    onehot = onehot_int.astype(jnp.float32)
    picked = jnp.sum(onehot * logits[:, None, :], axis=2)
    first_gate = jax.nn.sigmoid(picked[:, 0] - picked[:, 1])
    second_gate = jax.nn.sigmoid(picked[:, 1] - picked[:, 0])
    gate_values = jnp.stack([first_gate, second_gate], axis=1)
    gate_low = gate_values.astype(jnp.bfloat16)
    flat_hits = onehot_int.reshape(token_rows * choose_count, expert_count)
    before = jnp.cumsum(flat_hits, axis=0) - flat_hits
    slot_pos = jnp.sum(before * flat_hits, axis=1).reshape(token_rows, choose_count)
    slot_ids = jnp.arange(capacity, dtype=jnp.int32)
    dispatch_table = onehot[:, :, :, None] * (slot_pos[:, :, None, None] == slot_ids).astype(
        jnp.float32
    )
    slot_table = jnp.sum(dispatch_table, axis=1).astype(jnp.bfloat16)
    packed_grad = jnp.einsum(
        "rec,rd->ecd", slot_table, grad_output, preferred_element_type=jnp.float32
    ).astype(jnp.bfloat16)
    packed_gate = jnp.einsum("rkec,rk->ec", dispatch_table, gate_low.astype(jnp.float32)).astype(
        jnp.bfloat16
    )
    send_grad = jnp.repeat(packed_grad, spread, axis=0)
    send_gate = jnp.repeat(packed_gate, spread, axis=0)
    recv_grad, recv_gate = (
        lax.all_to_all(send_grad, ("expert", "tensor"), split_axis=0, concat_axis=0, tiled=True),
        lax.all_to_all(send_gate, ("expert", "tensor"), split_axis=0, concat_axis=0, tiled=True),
    )
    recv_grad = recv_grad.reshape(sources * capacity, model_width)
    recv_gate = recv_gate.reshape(sources * capacity).astype(jnp.float32)
    hidden_rows = hidden[0]
    gated_grad = (recv_gate[:, None] * recv_grad.astype(jnp.float32)).astype(jnp.bfloat16)
    expert_image = lax.dot_general(
        recv_grad, down_weight, (((1,), (1,)), ((), ())), preferred_element_type=jnp.float32
    )
    hidden_part = (recv_gate[:, None] * expert_image).astype(jnp.bfloat16)
    gate_partial = jnp.sum(hidden_rows.astype(jnp.float32) * expert_image, axis=1).reshape(
        sources, capacity
    )
    returned = lax.all_to_all(
        gate_partial, ("expert", "tensor"), split_axis=0, concat_axis=0, tiled=True
    )
    expert_sums = jnp.sum(returned.reshape(expert_count, spread, capacity), axis=1)
    gate_grad = jnp.einsum("rkec,ec->rk", dispatch_table, expert_sums)
    mixed_term = jnp.sum(gate_values * gate_grad, axis=1, keepdims=True)
    logit_part = gate_values * (gate_grad - mixed_term)
    logit_grad = jnp.sum(onehot * logit_part[:, :, None], axis=1)
    input_grad = jnp.dot(
        logit_grad, router_weight.astype(jnp.float32).T, precision=lax.Precision.HIGHEST
    ).astype(jnp.bfloat16)
    router_local = jnp.dot(
        full_input.astype(jnp.float32).T, logit_grad, precision=lax.Precision.HIGHEST
    )
    router_grad = lax.psum(router_local, ("dp", "expert", "tensor"))
    hidden_all = lax.all_to_all(hidden_rows, "dp", split_axis=1, concat_axis=0, tiled=True)
    gated_all = lax.all_gather(gated_grad, "dp", axis=0, tiled=True)
    weight_sum = lax.dot_general(
        hidden_all, gated_all, (((0,), (0,)), ((), ())), preferred_element_type=jnp.float32
    ).astype(jnp.bfloat16)
    return (weight_sum, hidden_part[None], router_grad, input_grad)


def solution(mesh):
    return jax.shard_map(
        per_device,
        mesh=mesh,
        in_specs=(
            P(("dp", "expert"), "tensor"),
            P(),
            P(("dp", "expert", "tensor"), None),
            P(("expert", "tensor"), None),
            P("dp", None, ("expert", "tensor")),
            P(("dp", "expert", "tensor"), None),
        ),
        out_specs=(
            P(("expert", "tensor", "dp"), None),
            P("dp", None, ("expert", "tensor")),
            P(),
            P(("dp", "expert", "tensor"), None),
        ),
        check_vma=False,
    )
```

profile of v0, /device:TPU:1, one launch (start us, length us, event | category | flops | bytes accessed | tf_op | source)
XLA Modules:
  0.0 211.5 jit_solution(2945085626296198110)
XLA Ops:
  8.0 3.5 %all-to-all-start = ((bf16[2,32,1024]{2,1,0:T(8,128)(2,1)}), bf16[2,32,1024]{2,1,0:T(8,128)(2,1)S(1)}, u32[]{:S(2)}, u32[]{:S(2)}) async-start(bf16[2,32,1024]{2,1,0:T(8,128)(2,1)} %bitcast.51), calls=%async_computation | async-start | bytes 262144 | tf_op jit(solution)/shard_map/all_to_all | solution.py:17
  11.5 0.8 copy.34
  13.7 1.7 all-to-all-done
  15.4 0.9 fusion.14
  16.3 0.7 multiply_reduce_fusion.2
  18.0 4.9 %all-to-all-start.1 = ((bf16[8,1,9]{2,1,0:T(2,128)(2,1)}), bf16[8,1,9]{2,1,0:T(2,128)(2,1)S(1)}, u32[]{:S(2)}, u32[]{:S(2)}) async-start(bf16[8,1,9]{2,1,0:T(2,128)(2,1)} %copy.37), calls=%async_computation.1 | async-start | bytes 8192 | tf_op jit(solution)/shard_map/all_to_all | solution.py:45
  22.8 1.1 convolution_convert_fusion
  23.9 4.2 %all-to-all-done.1 = bf16[8,1,9]{2,1,0:T(2,128)(2,1)S(1)} async-done(((bf16[8,1,9]{2,1,0:T(2,128)(2,1)}), bf16[8,1,9]{2,1,0:T(2,128)(2,1)S(1)}, u32[]{:S(2)}, u32[]{:S(2)}) %all-to-all-start.1) | async-done | bytes 176 | tf_op jit(solution)/shard_map/all_to_all | solution.py:45
  28.1 3.5 %all-to-all-start.2 = ((bf16[8,9,2048]{2,1,0:T(8,128)(2,1)}), bf16[8,9,2048]{2,1,0:T(8,128)(2,1)S(1)}, u32[]{:S(2)}, u32[]{:S(2)}) async-start(bf16[8,9,2048]{2,1,0:T(8,128)(2,1)} %convolution_convert_fusion), calls=%async_computation.2 | async-start | bytes 1048576 | tf_op jit(solution)/shard_map/all_to_all | solution.py:44
  31.7 10.3 %all-to-all-done.2 = bf16[8,9,2048]{2,1,0:T(8,128)(2,1)S(1)} async-done(((bf16[8,9,2048]{2,1,0:T(8,128)(2,1)}), bf16[8,9,2048]{2,1,0:T(8,128)(2,1)S(1)}, u32[]{:S(2)}, u32[]{:S(2)}) %all-to-all-start.2) | async-done | bytes 294944 | tf_op jit(solution)/shard_map/all_to_all | solution.py:44
  42.2 0.8 multiply_convert_fusion.1
  43.0 15.7 %fusion = (f32[72]{0:T(128)S(1)}, bf16[1,72,7680]{2,1,0:T(8,128)(2,1)}) fusion(bf16[1,72,7680]{2,1,0:T(8,128)(2,1)S(1)} %copy-done.1, f32[72]{0:T(128)S(1)} %reshape.61, bf16[72,2048]{1,0:T(8,128)(2,1)S(1)} %reshape.60, bf16[7680,2048]{1,0:T(8,128)(2,1)} %param.9), kind=kOutput, calls=%fused_computation.5 | convolution fusion | flops 2267688960 | bytes 33964608 | tf_op jit(solution)/shard_map/dot_general | solution.py:51
  58.8 0.7 all_to_all.54
  59.5 6.6 %all-to-all-start.4 = ((f32[8,1,9]{2,1,0:T(1,128)}), f32[8,1,9]{2,1,0:T(1,128)S(1)}, u32[]{:S(2)}, u32[]{:S(2)}) async-start(f32[8,1,9]{2,1,0:T(1,128)} %bitcast.13), calls=%async_computation.4 | async-start | bytes 8192 | tf_op jit(solution)/shard_map/all_to_all | solution.py:58
  66.4 1.1 copy.39
  67.5 3.8 %all-to-all-done.4 = f32[8,1,9]{2,1,0:T(1,128)S(1)} async-done(((f32[8,1,9]{2,1,0:T(1,128)}), f32[8,1,9]{2,1,0:T(1,128)S(1)}, u32[]{:S(2)}, u32[]{:S(2)}) %all-to-all-start.4) | async-done | bytes 320 | tf_op jit(solution)/shard_map/all_to_all | solution.py:58
  71.3 6.7 %all-to-all-start.3 = ((bf16[72,4,1920]{2,0,1:T(8,128)(2,1)}), bf16[72,4,1920]{2,0,1:T(8,128)(2,1)S(1)}, u32[]{:S(2)}, u32[]{:S(2)}) async-start(bf16[72,4,1920]{2,0,1:T(8,128)(2,1)} %copy.39), calls=%async_computation.3 | async-start | bytes 2211840 | tf_op jit(solution)/shard_map/all_to_all | solution.py:73
  78.2 0.8 convolution_bitcast_fusion
  79.1 1.0 convolution_convert_fusion.1
  80.0 12.1 %all-to-all-done.3 = bf16[72,4,1920]{2,0,1:T(8,128)(2,1)S(1)} async-done(((bf16[72,4,1920]{2,0,1:T(8,128)(2,1)}), bf16[72,4,1920]{2,0,1:T(8,128)(2,1)S(1)}, u32[]{:S(2)}, u32[]{:S(2)}) %all-to-all-start.3) | async-done | bytes 1105952 | tf_op jit(solution)/shard_map/all_to_all | solution.py:73
  92.1 8.0 %convert_bitcast_fusion = bf16[1920,2048]{0,1:T(8,128)(2,1)} fusion(bf16[288,2048]{1,0:T(8,128)(2,1)} %all-gather.2.cloned.1.call-done, bf16[288,1920]{1,0:T(8,128)(2,1)S(1)} %bitcast.49), kind=kOutput, calls=%fused_computation | convolution fusion | flops 2268856320 | bytes 10149888 | tf_op jit(solution)/shard_map/dot_general | solution.py:75
  100.1 10.6 %copy.41 = bf16[1920,2048]{1,0:T(8,128)(2,1)} copy(bf16[1920,2048]{0,1:T(8,128)(2,1)} %convert_bitcast_fusion) | data formatting | bytes 15728640
  110.7 91.9 %all-reduce.2.cloned.1.call-done = f32[2048,8]{0,1:T(8,128)} async-done(((f32[2048,8]{0,1:T(8,128)}), f32[2048,8]{0,1:T(8,128)}) %all-reduce.2.cloned.1.call-update) | async-done | bytes 65552 | tf_op jit(solution)/shard_map/psum | solution.py:72
  202.5 1.5 copy.56
  (38 shorter events, 3.2 us)
Async XLA Ops:
  8.0 14.8 %copy-start = (bf16[32,2048]{1,0:T(8,128)(2,1)S(1)}, bf16[32,2048]{1,0:T(8,128)(2,1)}, u32[]{:S(2)}) copy-start(bf16[32,2048]{1,0:T(8,128)(2,1)} %param.11) | copy-start | bytes 393220
  8.0 7.4 %all-to-all-start = ((bf16[2,32,1024]{2,1,0:T(8,128)(2,1)}), bf16[2,32,1024]{2,1,0:T(8,128)(2,1)S(1)}, u32[]{:S(2)}, u32[]{:S(2)}) async-start(bf16[2,32,1024]{2,1,0:T(8,128)(2,1)} %bitcast.51), calls=%async_computation | async-start | bytes 262144 | tf_op jit(solution)/shard_map/all_to_all | solution.py:17
  18.0 10.1 %all-to-all-start.1 = ((bf16[8,1,9]{2,1,0:T(2,128)(2,1)}), bf16[8,1,9]{2,1,0:T(2,128)(2,1)S(1)}, u32[]{:S(2)}, u32[]{:S(2)}) async-start(bf16[8,1,9]{2,1,0:T(2,128)(2,1)} %copy.37), calls=%async_computation.1 | async-start | bytes 8192 | tf_op jit(solution)/shard_map/all_to_all | solution.py:45
  23.9 19.1 %copy-start.1 = (bf16[1,72,7680]{2,1,0:T(8,128)(2,1)S(1)}, bf16[1,72,7680]{2,1,0:T(8,128)(2,1)}, u32[]{:S(2)}) copy-start(bf16[1,72,7680]{2,1,0:T(8,128)(2,1)} %param.10) | copy-start | bytes 3317764
  28.1 13.9 %all-to-all-start.2 = ((bf16[8,9,2048]{2,1,0:T(8,128)(2,1)}), bf16[8,9,2048]{2,1,0:T(8,128)(2,1)S(1)}, u32[]{:S(2)}, u32[]{:S(2)}) async-start(bf16[8,9,2048]{2,1,0:T(8,128)(2,1)} %convolution_convert_fusion), calls=%async_computation.2 | async-start | bytes 1048576 | tf_op jit(solution)/shard_map/all_to_all | solution.py:44
  31.6 60.5 %all-gather.2.cloned.1.call-start = ((), (), s32[]{:S(2)}) async-start(), calls=%async_computation.5 | async-start | bytes 1474560 | tf_op jit(solution)/shard_map/all_gather | solution.py:74
  59.5 11.9 %all-to-all-start.4 = ((f32[8,1,9]{2,1,0:T(1,128)}), f32[8,1,9]{2,1,0:T(1,128)S(1)}, u32[]{:S(2)}, u32[]{:S(2)}) async-start(f32[8,1,9]{2,1,0:T(1,128)} %bitcast.13), calls=%async_computation.4 | async-start | bytes 8192 | tf_op jit(solution)/shard_map/all_to_all | solution.py:58
  67.5 10.7 %copy-start.3 = (s32[32,2]{0,1:T(2,128)S(1)}, s32[32,2]{0,1:T(2,128)}, u32[]{:S(2)}) copy-start(s32[32,2]{0,1:T(2,128)} %param.8) | copy-start | bytes 772
  67.5 11.6 %copy-start.2 = (bf16[2048,8]{0,1:T(8,128)(2,1)S(1)}, bf16[2048,8]{0,1:T(8,128)(2,1)}, u32[]{:S(2)}) copy-start(bf16[2048,8]{0,1:T(8,128)(2,1)} %param.7) | copy-start | bytes 98308
  71.3 20.8 %all-to-all-start.3 = ((bf16[72,4,1920]{2,0,1:T(8,128)(2,1)}), bf16[72,4,1920]{2,0,1:T(8,128)(2,1)S(1)}, u32[]{:S(2)}, u32[]{:S(2)}) async-start(bf16[72,4,1920]{2,0,1:T(8,128)(2,1)} %copy.39), calls=%async_computation.3 | async-start | bytes 2211840 | tf_op jit(solution)/shard_map/all_to_all | solution.py:73
  78.0 124.6 %all-reduce.2.cloned.1.call-start = ((), (), s32[]{:S(2)}) async-start(), calls=%async_computation.6 | async-start | bytes 131072 | tf_op jit(solution)/shard_map/psum | solution.py:72
Sparse Core Ops, SparseCore 0:
  43.1 21.1 all-gather.1
Sparse Core Ops, SparseCore 1:
  84.6 117.9 all-reduce.1
where the time goes:
time: 212 us; the launch traced here: 211 us
  waiting for transfers between devices  124 us (58%)
  matrix products  27.6 us (13%)
  starting transfers between devices  25.2 us (12%)
  local copies, waits for them, and re-layouts  16.3 us (8%)
  between operations  15.6 us (7%)
  other arithmetic  2.78 us (1%)
    psum x1, waiting for transfers between devices, per_device(): router_grad = lax.psum(router_local, ('dp', 'expert', 'tensor'))  91.9 us
    dot_general x1, matrix products, per_device(): lax.dot_general(recv_grad, down_weight, (((1,), (1,)), ((), ())), preferr...  15.7 us
    unnamed x12, local copies, waits for them, and re-layouts  13 us
    all_to_all x1, waiting for transfers between devices, per_device(): lax.all_to_all(hidden_rows, 'dp', split_axis=1, concat_axis=0, tiled=True)  12.1 us
    all_to_all x1, waiting for transfers between devices, per_device(): lax.all_to_all(send_grad, ('expert', 'tensor'), split_axis=0, concat_axis...  10.3 us
    dot_general x1, matrix products, per_device(): lax.dot_general(hidden_all, gated_all, (((0,), (0,)), ((), ())), preferre...  7.96 us
    all_to_all x1, starting transfers between devices, per_device(): lax.all_to_all(hidden_rows, 'dp', split_axis=1, concat_axis=0, tiled=True)  6.66 us
    all_to_all x1, starting transfers between devices, per_device(): lax.all_to_all(gate_partial, ('expert', 'tensor'), split_axis=0, concat_a...  6.6 us
  transfers between devices with their start and end apart: 7, of which 6 were waited for; matrix products, arithmetic and copies ran while one was open for 19% of the time, Pallas kernels for 0%

commit v1 on v0

--- a/solution.py
+++ b/solution.py
@@ -69,7 +69,7 @@
     router_local = jnp.dot(
         full_input.astype(jnp.float32).T, logit_grad, precision=lax.Precision.HIGHEST
     )
-    router_grad = lax.psum(router_local, ("dp", "expert", "tensor"))
+    router_grad = jnp.sum(lax.all_gather(router_local, ("dp", "expert", "tensor")), axis=0)
     hidden_all = lax.all_to_all(hidden_rows, "dp", split_axis=1, concat_axis=0, tiled=True)
     gated_all = lax.all_gather(gated_grad, "dp", axis=0, tiled=True)
     weight_sum = lax.dot_general(

time: 212 us -> 138 us (0.65)
  waiting for transfers between devices: 124 us -> 45.4 us
  blocking collectives: 0 us -> 11.7 us
  starting transfers between devices: 25.2 us -> 18.6 us
  other arithmetic: 2.78 us -> 5.11 us
    psum x1 -> x0, waiting for transfers between devices: 91.9 us -> none  [per_device(): router_grad = lax.psum(router_local, ('dp', 'expert', 'tensor'))]
    all_gather x0 -> x1, waiting for transfers between devices: none -> 15.5 us  [per_device(): lax.all_gather(router_local, ('dp', 'expert', 'tensor'))]
    all_to_all x0 -> x1, blocking collectives: none -> 11.7 us  [per_device(): lax.all_to_all(gate_partial, ('expert', 'tensor'), split_axis=0, concat_a...]
    all_to_all x1 -> x0, starting transfers between devices: 6.6 us -> none  [per_device(): lax.all_to_all(gate_partial, ('expert', 'tensor'), split_axis=0, concat_a...]
    all_to_all x1 -> x0, waiting for transfers between devices: 3.84 us -> none  [per_device(): lax.all_to_all(gate_partial, ('expert', 'tensor'), split_axis=0, concat_a...]
    reduce_sum x0 -> x1, other arithmetic: none -> 2.33 us  [per_device(): jnp.sum(lax.all_gather(router_local, ('dp', 'expert', 'tensor')), axis=0)]
    unnamed x12 -> x11, local copies, waits for them, and re-layouts: 13 us -> 11.5 us
  transfers between devices with their start and end apart: 7 -> 6, of which waited for: 6 -> 5; matrix products, arithmetic and copies ran while one was open for 19% -> 30% of each run, Pallas kernels for 0% -> 0%
where the time goes in v1:
time: 138 us; the launch traced here: 137 us
  waiting for transfers between devices  45.4 us (33%)
  matrix products  27.6 us (20%)
  starting transfers between devices  18.6 us (13%)
  local copies, waits for them, and re-layouts  14.2 us (10%)
  between operations  14.2 us (10%)
  blocking collectives  11.7 us (8%)
  other arithmetic  5.11 us (4%)
    dot_general x1, matrix products, per_device(): lax.dot_general(recv_grad, down_weight, (((1,), (1,)), ((), ())), preferr...  15.7 us
    all_gather x1, waiting for transfers between devices, per_device(): lax.all_gather(router_local, ('dp', 'expert', 'tensor'))  15.5 us
    all_to_all x1, waiting for transfers between devices, per_device(): lax.all_to_all(hidden_rows, 'dp', split_axis=1, concat_axis=0, tiled=True)  13.6 us
    all_to_all x1, blocking collectives, per_device(): lax.all_to_all(gate_partial, ('expert', 'tensor'), split_axis=0, concat_a...  11.7 us
    unnamed x11, local copies, waits for them, and re-layouts  11.5 us
    all_to_all x1, waiting for transfers between devices, per_device(): lax.all_to_all(send_grad, ('expert', 'tensor'), split_axis=0, concat_axis...  10.3 us
    dot_general x1, matrix products, per_device(): lax.dot_general(hidden_all, gated_all, (((0,), (0,)), ((), ())), preferre...  7.96 us
    all_to_all x1, starting transfers between devices, per_device(): lax.all_to_all(hidden_rows, 'dp', split_axis=1, concat_axis=0, tiled=True)  6.66 us
  transfers between devices with their start and end apart: 6, of which 5 were waited for; matrix products, arithmetic and copies ran while one was open for 30% of the time, Pallas kernels for 0%

profile of v1, /device:TPU:1, one launch (start us, length us, event | category | flops | bytes accessed | tf_op | source)
XLA Modules:
  0.0 136.9 jit_solution(5524990726157091216)
XLA Ops:
  7.2 3.5 %all-to-all-start = ((bf16[2,32,1024]{2,1,0:T(8,128)(2,1)}), bf16[2,32,1024]{2,1,0:T(8,128)(2,1)S(1)}, u32[]{:S(2)}, u32[]{:S(2)}) async-start(bf16[2,32,1024]{2,1,0:T(8,128)(2,1)} %bitcast.53), calls=%async_computation | async-start | bytes 262144 | tf_op jit(solution)/shard_map/all_to_all | solution.py:17
  10.7 0.8 copy.34
  11.5 0.7 convert_convert_fusion
  12.8 1.7 %all-to-all-done = bf16[2,32,1024]{2,1,0:T(8,128)(2,1)S(1)} async-done(((bf16[2,32,1024]{2,1,0:T(8,128)(2,1)}), bf16[2,32,1024]{2,1,0:T(8,128)(2,1)S(1)}, u32[]{:S(2)}, u32[]{:S(2)}) %all-to-all-start) | async-done | bytes 131104 | tf_op jit(solution)/shard_map/all_to_all | solution.py:17
  14.6 0.9 fusion.14
  15.5 0.7 multiply_reduce_fusion.2
  16.5 0.6 copy.37
  17.1 4.9 %all-to-all-start.1 = ((bf16[8,1,9]{2,1,0:T(2,128)(2,1)}), bf16[8,1,9]{2,1,0:T(2,128)(2,1)S(1)}, u32[]{:S(2)}, u32[]{:S(2)}) async-start(bf16[8,1,9]{2,1,0:T(2,128)(2,1)} %copy.37), calls=%async_computation.1 | async-start | bytes 8192 | tf_op jit(solution)/shard_map/all_to_all | solution.py:45
  22.0 1.1 convolution_convert_fusion
  23.1 4.2 %all-to-all-done.1 = bf16[8,1,9]{2,1,0:T(2,128)(2,1)S(1)} async-done(((bf16[8,1,9]{2,1,0:T(2,128)(2,1)}), bf16[8,1,9]{2,1,0:T(2,128)(2,1)S(1)}, u32[]{:S(2)}, u32[]{:S(2)}) %all-to-all-start.1) | async-done | bytes 176 | tf_op jit(solution)/shard_map/all_to_all | solution.py:45
  27.3 3.5 %all-to-all-start.2 = ((bf16[8,9,2048]{2,1,0:T(8,128)(2,1)}), bf16[8,9,2048]{2,1,0:T(8,128)(2,1)S(1)}, u32[]{:S(2)}, u32[]{:S(2)}) async-start(bf16[8,9,2048]{2,1,0:T(8,128)(2,1)} %convolution_convert_fusion), calls=%async_computation.2 | async-start | bytes 1048576 | tf_op jit(solution)/shard_map/all_to_all | solution.py:44
  30.9 10.3 %all-to-all-done.2 = bf16[8,9,2048]{2,1,0:T(8,128)(2,1)S(1)} async-done(((bf16[8,9,2048]{2,1,0:T(8,128)(2,1)}), bf16[8,9,2048]{2,1,0:T(8,128)(2,1)S(1)}, u32[]{:S(2)}, u32[]{:S(2)}) %all-to-all-start.2) | async-done | bytes 294944 | tf_op jit(solution)/shard_map/all_to_all | solution.py:44
  41.3 0.8 multiply_convert_fusion.1
  42.3 15.7 %fusion = (f32[72]{0:T(128)S(1)}, bf16[1,72,7680]{2,1,0:T(8,128)(2,1)}) fusion(bf16[1,72,7680]{2,1,0:T(8,128)(2,1)S(1)} %copy-done.1, f32[72]{0:T(128)S(1)} %reshape.61, bf16[72,2048]{1,0:T(8,128)(2,1)S(1)} %reshape.60, bf16[7680,2048]{1,0:T(8,128)(2,1)} %param.9), kind=kOutput, calls=%fused_computation.5 | convolution fusion | flops 2267688960 | bytes 33964608 | tf_op jit(solution)/shard_map/dot_general | solution.py:51
  58.1 11.7 %all_to_all.61 = f32[8,1,9]{2,1,0:T(1,128)S(1)} all-to-all(f32[8,1,9]{2,1,0:T(1,128)S(1)} %bitcast.55), channel_id=1, replica_groups=mesh['dp'=4,'expert'=4,'tensor'=2] {'expert','tensor'}, dimensions={0} | all-to-all | bytes 576 | tf_op jit(solution)/shard_map/all_to_all | solution.py:58
  70.1 0.8 convolution_bitcast_fusion
  71.2 1.1 copy.39
  72.3 6.7 %all-to-all-start.3 = ((bf16[72,4,1920]{2,0,1:T(8,128)(2,1)}), bf16[72,4,1920]{2,0,1:T(8,128)(2,1)S(1)}, u32[]{:S(2)}, u32[]{:S(2)}) async-start(bf16[72,4,1920]{2,0,1:T(8,128)(2,1)} %copy.39), calls=%async_computation.3 | async-start | bytes 2211840 | tf_op jit(solution)/shard_map/all_to_all | solution.py:73
  79.0 1.0 convolution_convert_fusion.1
  80.0 13.6 %all-to-all-done.3 = bf16[72,4,1920]{2,0,1:T(8,128)(2,1)S(1)} async-done(((bf16[72,4,1920]{2,0,1:T(8,128)(2,1)}), bf16[72,4,1920]{2,0,1:T(8,128)(2,1)S(1)}, u32[]{:S(2)}, u32[]{:S(2)}) %all-to-all-start.3) | async-done | bytes 1105952 | tf_op jit(solution)/shard_map/all_to_all | solution.py:73
  93.6 8.0 %convert_bitcast_fusion = bf16[1920,2048]{0,1:T(8,128)(2,1)} fusion(bf16[288,2048]{1,0:T(8,128)(2,1)} %all-gather.4.cloned.1.call-done, bf16[288,1920]{1,0:T(8,128)(2,1)S(1)} %bitcast.51), kind=kOutput, calls=%fused_computation | convolution fusion | flops 2268856320 | bytes 10149888 | tf_op jit(solution)/shard_map/dot_general | solution.py:75
  101.6 10.6 %copy.41 = bf16[1920,2048]{1,0:T(8,128)(2,1)} copy(bf16[1920,2048]{0,1:T(8,128)(2,1)} %convert_bitcast_fusion) | data formatting | bytes 15728640
  112.2 15.5 %all-gather.6.cloned.1.call-done = f32[65536,8]{0,1:T(8,128)} async-done(((f32[2048,8]{0,1:T(8,128)}), f32[65536,8]{0,1:T(8,128)}) %all-gather.6.cloned.1.call-update) | async-done | bytes 2097168 | tf_op jit(solution)/shard_map/all_gather | solution.py:72
  127.7 2.3 %reduce_sum.76 = f32[2048,8]{0,1:T(8,128)} reduce(f32[32,2048,8]{1,2,0:T(8,128)} %bitcast.48, f32[]{:T(128)} %constant.9.clone.1), dimensions={0}, to_apply=%region_7.8 | reduce | flops 507904 | bytes 2162692 | tf_op jit(solution)/shard_map/reduce_sum | solution.py:72
  (37 shorter events, 2.0 us)
Async XLA Ops:
  7.2 14.8 %copy-start = (bf16[32,2048]{1,0:T(8,128)(2,1)S(1)}, bf16[32,2048]{1,0:T(8,128)(2,1)}, u32[]{:S(2)}) copy-start(bf16[32,2048]{1,0:T(8,128)(2,1)} %param.11) | copy-start | bytes 393220
  7.2 7.4 %all-to-all-start = ((bf16[2,32,1024]{2,1,0:T(8,128)(2,1)}), bf16[2,32,1024]{2,1,0:T(8,128)(2,1)S(1)}, u32[]{:S(2)}, u32[]{:S(2)}) async-start(bf16[2,32,1024]{2,1,0:T(8,128)(2,1)} %bitcast.53), calls=%async_computation | async-start | bytes 262144 | tf_op jit(solution)/shard_map/all_to_all | solution.py:17
  12.3 30.0 %copy-start.1 = (bf16[1,72,7680]{2,1,0:T(8,128)(2,1)S(1)}, bf16[1,72,7680]{2,1,0:T(8,128)(2,1)}, u32[]{:S(2)}) copy-start(bf16[1,72,7680]{2,1,0:T(8,128)(2,1)} %param.10) | copy-start | bytes 3317764
  17.1 10.1 %all-to-all-start.1 = ((bf16[8,1,9]{2,1,0:T(2,128)(2,1)}), bf16[8,1,9]{2,1,0:T(2,128)(2,1)S(1)}, u32[]{:S(2)}, u32[]{:S(2)}) async-start(bf16[8,1,9]{2,1,0:T(2,128)(2,1)} %copy.37), calls=%async_computation.1 | async-start | bytes 8192 | tf_op jit(solution)/shard_map/all_to_all | solution.py:45
  27.3 13.9 %all-to-all-start.2 = ((bf16[8,9,2048]{2,1,0:T(8,128)(2,1)}), bf16[8,9,2048]{2,1,0:T(8,128)(2,1)S(1)}, u32[]{:S(2)}, u32[]{:S(2)}) async-start(bf16[8,9,2048]{2,1,0:T(8,128)(2,1)} %convolution_convert_fusion), calls=%async_computation.2 | async-start | bytes 1048576 | tf_op jit(solution)/shard_map/all_to_all | solution.py:44
  30.8 62.8 %all-gather.4.cloned.1.call-start = ((), (), s32[]{:S(2)}) async-start(), calls=%async_computation.5 | async-start | bytes 1474560 | tf_op jit(solution)/shard_map/all_gather | solution.py:74
  42.2 27.8 %copy-start.3 = (s32[32,2]{0,1:T(2,128)S(1)}, s32[32,2]{0,1:T(2,128)}, u32[]{:S(2)}) copy-start(s32[32,2]{0,1:T(2,128)} %param.8) | copy-start | bytes 772
  42.2 85.5 %all-gather.6.cloned.1.call-start = ((), (), s32[]{:S(2)}) async-start(), calls=%async_computation.6 | async-start | bytes 2162688 | tf_op jit(solution)/shard_map/all_gather | solution.py:72
  71.2 7.8 %copy-start.2 = (bf16[2048,8]{0,1:T(8,128)(2,1)S(1)}, bf16[2048,8]{0,1:T(8,128)(2,1)}, u32[]{:S(2)}) copy-start(bf16[2048,8]{0,1:T(8,128)(2,1)} %param.7) | copy-start | bytes 98308
  72.3 21.3 %all-to-all-start.3 = ((bf16[72,4,1920]{2,0,1:T(8,128)(2,1)}), bf16[72,4,1920]{2,0,1:T(8,128)(2,1)S(1)}, u32[]{:S(2)}, u32[]{:S(2)}) async-start(bf16[72,4,1920]{2,0,1:T(8,128)(2,1)} %copy.39), calls=%async_computation.3 | async-start | bytes 2211840 | tf_op jit(solution)/shard_map/all_to_all | solution.py:73
Sparse Core Ops, SparseCore 0:
  42.3 21.1 all-gather.3
  71.0 56.6 all-gather.5
